TPU v7x, 32 devices: a whole 2x2x4 slice. The times are simulated.
32 devices in a mesh: expert: 8 (over z, x), shard: 4 (over y, core).
Axes of the slice: x: 2, y: 2, z: 4, core: 2. Of those that a mesh axis runs over, the one named last changes fastest.
Arguments:
- train_down: float32 [16, 6400, 4096], P('expert', None, 'shard'), may hold values from -0.109375 to 0.109375
- router_weight: float32 [4096, 16], P('shard', 'expert'), may hold values from -0.09375 to 0.09375
- router_gain: float32 [4096], P('shard'), may hold values from 0.25 to 1.75
Outputs:
- ready_down: bfloat16 [16, 6400, 4096], P('expert', 'shard')
- scale_down: float32 [16, 6400], P('expert', 'shard')
- serve_router: bfloat16 [4096, 16], replicated
All inputs are finite; a program needn't handle non-finite values. Where the computation divides by a largest or mean magnitude, that divisor is 1e-20 or more.
Results may differ from a plain program's by a relative error of at most 0.001.
Values may be sent and summed in bfloat16 or wider, within the bound.
A program may use at most 192 MiB of HBM per device.

v0:
```python
import jax
import jax.numpy as jnp
from jax import lax
from jax.sharding import PartitionSpec as P


def per_device(train_down, router_weight, router_gain):
    scale_down = lax.pmax(jnp.max(jnp.abs(train_down), axis=2), "shard")
    narrow_down = (train_down / jnp.expand_dims(scale_down, 2)).astype(jnp.bfloat16)
    ready_down = lax.all_to_all(narrow_down, "shard", split_axis=1, concat_axis=2, tiled=True)
    scale_down = lax.dynamic_slice_in_dim(
        scale_down, lax.axis_index("shard") * ready_down.shape[1], ready_down.shape[1], axis=1
    )
    part_router = (router_weight * router_gain[:, None]).astype(jnp.bfloat16)
    row_router = lax.all_gather(part_router, "shard", axis=0, tiled=True)
    serve_router = lax.all_gather(row_router, "expert", axis=1, tiled=True)
    return (ready_down, scale_down, serve_router)


def solution(mesh):
    in_specs = (P("expert", None, "shard"), P("shard", "expert"), P("shard"))
    out_specs = (P("expert", "shard", None), P("expert", "shard"), P())
    return jax.shard_map(
        per_device, mesh=mesh, in_specs=in_specs, out_specs=out_specs, check_vma=False
    )
```

profile of v0, /device:TPU:0, one launch (start us, length us, event | category | flops | bytes accessed | tf_op | source)
XLA Modules:
  0.0 506.3 jit_solution(6970151837764628725)
XLA Ops:
  0.6 17.0 %abs_reduce_fusion = f32[2,6400]{1,0:T(2,128)S(1)} fusion(f32[2,6400,1024]{2,1,0:T(8,128)} %param.3), kind=kLoop, calls=%fused_computation.1 | loop fusion | flops 26201600 | bytes 52480000 | tf_op jit(solution)/shard_map/reduce_max | solution.py:8
  17.6 13.4 %pmax.7 = f32[2,6400]{1,0:T(2,128)S(1)} all-reduce(f32[2,6400]{1,0:T(2,128)S(1)} %abs_reduce_fusion), channel_id=1, replica_groups=mesh['expert'=8,'shard'=4] {'shard'}, use_global_device_ids=true, to_apply=%region_1.0 | all-reduce | flops 12800 | bytes 102400 | tf_op jit(solution)/shard_map/pmax | solution.py:8
  31.1 26.1 %divide_convert_fusion = bf16[2,6400,1024]{2,1,0:T(8,128)(2,1)} fusion(f32[2,6400,1024]{2,1,0:T(8,128)} %param.3, f32[2,6400]{1,0:T(2,128)S(1)} %pmax.7), kind=kLoop, calls=%fused_computation | loop fusion | flops 26214400 | bytes 78694400 | tf_op jit(solution)/shard_map/convert_element_type | solution.py:9
  57.2 0.0 copy-start
  57.2 0.0 copy-start.1
  57.2 47.4 %copy.10 = bf16[2,6400,1024]{2,0,1:T(2,128)(2,1)} copy(bf16[2,6400,1024]{2,1,0:T(8,128)(2,1)} %divide_convert_fusion) | data formatting | bytes 52428800 | tf_op jit(solution)/shard_map/convert_element_type | solution.py:9
  104.6 8.6 %all-to-all-start = ((bf16[2,6400,1024]{2,0,1:T(2,128)(2,1)}), bf16[2,6400,1024]{2,0,1:T(2,128)(2,1)}, u32[]{:S(2)}, u32[]{:S(2)}) async-start(bf16[2,6400,1024]{2,0,1:T(2,128)(2,1)} %copy.10), calls=%async_computation | async-start | bytes 52428800 | tf_op jit(solution)/shard_map/all_to_all | solution.py:10
  113.2 0.0 copy-done
  113.2 0.0 copy-done.1
  113.2 285.0 %all_gather.6 = bf16[4096,2]{0,1:T(2,128)(2,1)S(1)} all-gather(bf16[1024,2]{0,1:T(2,128)(2,1)S(1)} %multiply_convert_fusion), channel_id=1, replica_groups=mesh['expert'=8,'shard'=4] {'shard'}, dimensions={0}, use_global_device_ids=true | all-gather | bytes 20480 | tf_op jit(solution)/shard_map/all_gather | solution.py:15
  398.2 30.8 %all-gather = bf16[8,2,4096]{2,1,0:T(2,128)(2,1)S(1)} all-gather(bf16[1,2,4096]{2,1,0:T(2,128)(2,1)S(1)} %bitcast.8), channel_id=1, replica_groups=mesh['expert'=8,'shard'=4] {'expert'}, dimensions={0}, use_global_device_ids=true | all-gather | bytes 147456 | tf_op jit(solution)/shard_map/all_gather | solution.py:16
  429.1 0.7 reshape.9
  429.8 0.7 constant_dynamic-slice_fusion
  430.5 0.0 all-to-all-done
  430.5 33.4 %copy.11 = bf16[2,1600,4,1024]{3,2,1,0:T(4,128)(2,1)} copy(bf16[2,1600,4,1024]{3,0,1,2:T(2,128)(2,1)} %bitcast.1) | data formatting | bytes 52428800 | tf_op jit(solution)/shard_map/all_to_all | solution.py:10
  463.8 42.5 %all_to_all.16 = bf16[2,1600,4096]{2,1,0:T(8,128)(2,1)} reshape(bf16[2,1600,4,1024]{3,2,1,0:T(4,128)(2,1)} %copy.11) | data formatting | bytes 52428800 | tf_op jit(solution)/shard_map/all_to_all | solution.py:10
  (1 shorter events, 0.0 us)
Async XLA Ops:
  57.2 56.0 %copy-start = (f32[1024,2]{0,1:T(2,128)S(1)}, f32[1024,2]{0,1:T(2,128)}, u32[]{:S(2)}) copy-start(f32[1024,2]{0,1:T(2,128)} %param.4) | copy-start | bytes 24580
  57.2 56.0 %copy-start.1 = (f32[1024]{0:T(1024)S(1)}, f32[1024]{0:T(1024)}, u32[]{:S(2)}) copy-start(f32[1024]{0:T(1024)} %param.5) | copy-start | bytes 12292
  104.6 325.9 %all-to-all-start = ((bf16[2,6400,1024]{2,0,1:T(2,128)(2,1)}), bf16[2,6400,1024]{2,0,1:T(2,128)(2,1)}, u32[]{:S(2)}, u32[]{:S(2)}) async-start(bf16[2,6400,1024]{2,0,1:T(2,128)(2,1)} %copy.10), calls=%async_computation | async-start | bytes 52428800 | tf_op jit(solution)/shard_map/all_to_all | solution.py:10
where the time goes:
time: 508 us; the launch traced here: 506 us
  blocking collectives  329 us (65%)
  local copies, waits for them, and re-layouts  125 us (25%)
  other arithmetic  43.2 us (9%)
  starting transfers between devices  8.59 us (2%)
    all_gather x1, blocking collectives, per_device(): row_router = lax.all_gather(part_router, 'shard', axis=0, tiled=True)  285 us
    all_to_all x2, local copies, waits for them, and re-layouts, per_device(): lax.all_to_all(narrow_down, 'shard', split_axis=1, concat_axis=2, tiled=T...  75.8 us
    convert_element_type x1, local copies, waits for them, and re-layouts, per_device(): (train_down / jnp.expand_dims(scale_down, 2)).astype(jnp.bfloat16)  47.4 us
    all_gather x1, blocking collectives, per_device(): serve_router = lax.all_gather(row_router, 'expert', axis=1, tiled=True)  30.8 us
    convert_element_type x1, other arithmetic, per_device(): (train_down / jnp.expand_dims(scale_down, 2)).astype(jnp.bfloat16)  26.1 us
    reduce_max x1, other arithmetic, per_device(): scale_down = lax.pmax(jnp.max(jnp.abs(train_down), axis=2), 'shard')  17 us
    pmax x1, blocking collectives, per_device(): scale_down = lax.pmax(jnp.max(jnp.abs(train_down), axis=2), 'shard')  13.4 us
  transfers between devices with their start and end apart: 1, of which 0 were waited for; matrix products, arithmetic and copies ran while one was open for 0% of the time, Pallas kernels for 0%

commit v1 on v0

--- a/solution.py
+++ b/solution.py
@@ -7,7 +7,12 @@
 def per_device(train_down, router_weight, router_gain):
     scale_down = lax.pmax(jnp.max(jnp.abs(train_down), axis=2), "shard")
     narrow_down = (train_down / jnp.expand_dims(scale_down, 2)).astype(jnp.bfloat16)
-    ready_down = lax.all_to_all(narrow_down, "shard", split_axis=1, concat_axis=2, tiled=True)
+    ready_down = jnp.concatenate(
+        lax.all_to_all(
+            jnp.stack(jnp.split(narrow_down, lax.axis_size("shard"), axis=1)), "shard", 0, 0
+        ),
+        axis=2,
+    )
     scale_down = lax.dynamic_slice_in_dim(
         scale_down, lax.axis_index("shard") * ready_down.shape[1], ready_down.shape[1], axis=1
     )

time: 508 us -> 425 us (0.84)
  local copies, waits for them, and re-layouts: 125 us -> 32.6 us
  other arithmetic: 43.2 us -> 53.7 us
    all_to_all x2 -> x0, local copies, waits for them, and re-layouts: 75.8 us -> none  [per_device(): lax.all_to_all(narrow_down, 'shard', split_axis=1, concat_axis=2, tiled=T...]
    convert_element_type x1 -> x0, local copies, waits for them, and re-layouts: 47.4 us -> none  [per_device(): (train_down / jnp.expand_dims(scale_down, 2)).astype(jnp.bfloat16)]
    reshape x0 -> x1, local copies, waits for them, and re-layouts: none -> 21.7 us  [per_device(): jnp.concatenate(lax.all_to_all(jnp.stack(jnp.split(narrow_down, lax.axis_...]
    another operation x0 -> x1, other arithmetic: none -> 10.5 us  [per_device(): jnp.stack(jnp.split(narrow_down, lax.axis_size('shard'), axis=1))]
    another operation x0 -> x1, local copies, waits for them, and re-layouts: none -> 9.52 us  [per_device(): jnp.stack(jnp.split(narrow_down, lax.axis_size('shard'), axis=1))]
where the time goes in v1:
time: 425 us
  blocking collectives  329 us (77%)
  other arithmetic  53.7 us (13%)
  local copies, waits for them, and re-layouts  32.6 us (8%)
  starting transfers between devices  8.72 us (2%)
    all_gather x1, blocking collectives, per_device(): row_router = lax.all_gather(part_router, 'shard', axis=0, tiled=True)  285 us
    all_gather x1, blocking collectives, per_device(): serve_router = lax.all_gather(row_router, 'expert', axis=1, tiled=True)  30.8 us
    convert_element_type x1, other arithmetic, per_device(): (train_down / jnp.expand_dims(scale_down, 2)).astype(jnp.bfloat16)  26.1 us
    reshape x1, local copies, waits for them, and re-layouts, per_device(): jnp.concatenate(lax.all_to_all(jnp.stack(jnp.split(narrow_down, lax.axis_...  21.7 us
    reduce_max x1, other arithmetic, per_device(): scale_down = lax.pmax(jnp.max(jnp.abs(train_down), axis=2), 'shard')  17 us
    pmax x1, blocking collectives, per_device(): scale_down = lax.pmax(jnp.max(jnp.abs(train_down), axis=2), 'shard')  13.4 us
    another operation x1, other arithmetic, per_device(): jnp.stack(jnp.split(narrow_down, lax.axis_size('shard'), axis=1))  10.5 us
    another operation x1, local copies, waits for them, and re-layouts, per_device(): jnp.stack(jnp.split(narrow_down, lax.axis_size('shard'), axis=1))  9.52 us
  transfers between devices with their start and end apart: 1, of which 0 were waited for; matrix products, arithmetic and copies ran while one was open for 0% of the time, Pallas kernels for 0%

profile of v1, /device:TPU:0, one launch (start us, length us, event | category | flops | bytes accessed | tf_op | source)
XLA Modules:
  0.0 425.0 jit_solution(13586044077871705649)
XLA Ops:
  0.6 17.0 %abs_reduce_fusion = f32[2,6400]{1,0:T(2,128)S(1)} fusion(f32[2,6400,1024]{2,1,0:T(8,128)} %param.3), kind=kLoop, calls=%fused_computation.1 | loop fusion | flops 26201600 | bytes 52480000 | tf_op jit(solution)/shard_map/reduce_max | solution.py:8
  17.6 13.4 %pmax.7 = f32[2,6400]{1,0:T(2,128)S(1)} all-reduce(f32[2,6400]{1,0:T(2,128)S(1)} %abs_reduce_fusion), channel_id=1, replica_groups=mesh['expert'=8,'shard'=4] {'shard'}, use_global_device_ids=true, to_apply=%region_1.0 | all-reduce | flops 12800 | bytes 102400 | tf_op jit(solution)/shard_map/pmax | solution.py:8
  31.1 26.1 %divide_convert_fusion = bf16[2,6400,1024]{2,1,0:T(8,128)(2,1)} fusion(f32[2,6400,1024]{2,1,0:T(8,128)} %param.3, f32[2,6400]{1,0:T(2,128)S(1)} %pmax.7), kind=kLoop, calls=%fused_computation | loop fusion | flops 26214400 | bytes 78694400 | tf_op jit(solution)/shard_map/convert_element_type | solution.py:9
  57.2 9.5 %slice_bitcast_fusion.3 = (bf16[1,2,1600,1024]{3,2,1,0:T(8,128)(2,1)S(1)}, bf16[1,2,1600,1024]{3,2,1,0:T(8,128)(2,1)S(1)}, bf16[1,2,1600,1024]{3,2,1,0:T(8,128)(2,1)S(1)}, bf16[1,2,1600,1024]{3,2,1,0:T(8,128)(2,1)S(1)}) fusion(bf16[2,6400,1024]{2,1,0:T(8,128)(2,1)} %divide_convert_fusion), kind=kLoop, calls=%fused_computation.6 | loop fusion | bytes 52428800 | tf_op jit(solution)/shard_map/stack | solution.py:12
  66.7 10.5 %pad_maximum_fusion = bf16[4,2,1600,1024]{3,2,1,0:T(8,128)(2,1)} fusion(bf16[1,2,1600,1024]{3,2,1,0:T(8,128)(2,1)S(1)} %get-tuple-element.4, bf16[1,2,1600,1024]{3,2,1,0:T(8,128)(2,1)S(1)} %get-tuple-element.5, bf16[1,2,1600,1024]{3,2,1,0:T(8,128)(2,1)S(1)} %get-tuple-element.6, bf16[1,2,1600,1024]{3,2,1,0:T(8,128)(2,1)S(1)} %get-tuple-element.3), kind=kLoop, calls=%fused_computation.2 | loop fusion | flops 39321600 | bytes 52428800 | tf_op jit(solution)/shard_map/stack | solution.py:12
  77.3 0.0 copy-start
  77.3 0.0 copy-start.1
  77.3 8.7 %all-to-all-start = ((bf16[4,2,1600,1024]{3,2,1,0:T(8,128)(2,1)}), bf16[4,2,1600,1024]{3,2,1,0:T(8,128)(2,1)}, u32[]{:S(2)}, u32[]{:S(2)}) async-start(bf16[4,2,1600,1024]{3,2,1,0:T(8,128)(2,1)} %pad_maximum_fusion), calls=%async_computation | async-start | bytes 52428800 | tf_op jit(solution)/shard_map/all_to_all | solution.py:11
  86.0 0.0 copy-done
  86.0 0.0 copy-done.1
  86.0 285.0 %all_gather.6 = bf16[4096,2]{0,1:T(2,128)(2,1)S(1)} all-gather(bf16[1024,2]{0,1:T(2,128)(2,1)S(1)} %multiply_convert_fusion), channel_id=1, replica_groups=mesh['expert'=8,'shard'=4] {'shard'}, dimensions={0}, use_global_device_ids=true | all-gather | bytes 20480 | tf_op jit(solution)/shard_map/all_gather | solution.py:20
  371.0 30.8 %all-gather = bf16[8,2,4096]{2,1,0:T(2,128)(2,1)S(1)} all-gather(bf16[1,2,4096]{2,1,0:T(2,128)(2,1)S(1)} %bitcast.17), channel_id=1, replica_groups=mesh['expert'=8,'shard'=4] {'expert'}, dimensions={0}, use_global_device_ids=true | all-gather | bytes 147456 | tf_op jit(solution)/shard_map/all_gather | solution.py:21
  401.9 0.7 reshape.17
  402.6 0.7 constant_dynamic-slice_fusion
  403.3 0.0 all-to-all-done
  403.3 21.7 %copy.8 = bf16[4,2,200,8,1024]{4,3,0,2,1:T(8,128)(2,1)} copy(bf16[4,2,200,8,1024]{4,3,2,1,0:T(8,128)(2,1)} %bitcast.9) | data formatting | bytes 52428800 | tf_op jit(solution)/shard_map/reshape | solution.py:10
  (1 shorter events, 0.0 us)
Async XLA Ops:
  77.3 8.7 %copy-start = (f32[1024,2]{0,1:T(2,128)S(1)}, f32[1024,2]{0,1:T(2,128)}, u32[]{:S(2)}) copy-start(f32[1024,2]{0,1:T(2,128)} %param.4) | copy-start | bytes 24580
  77.3 8.7 %copy-start.1 = (f32[1024]{0:T(1024)S(1)}, f32[1024]{0:T(1024)}, u32[]{:S(2)}) copy-start(f32[1024]{0:T(1024)} %param.5) | copy-start | bytes 12292
  77.3 326.0 %all-to-all-start = ((bf16[4,2,1600,1024]{3,2,1,0:T(8,128)(2,1)}), bf16[4,2,1600,1024]{3,2,1,0:T(8,128)(2,1)}, u32[]{:S(2)}, u32[]{:S(2)}) async-start(bf16[4,2,1600,1024]{3,2,1,0:T(8,128)(2,1)} %pad_maximum_fusion), calls=%async_computation | async-start | bytes 52428800 | tf_op jit(solution)/shard_map/all_to_all | solution.py:11

commit v2 on v0

--- a/solution.py
+++ b/solution.py
@@ -2,6 +2,12 @@
 import jax.numpy as jnp
 from jax import lax
 from jax.sharding import PartitionSpec as P
+
+
+def tiled_gather(x, axis, dim):
+    size = lax.axis_size(axis)
+    repeats = [size if d == dim else 1 for d in range(x.ndim)]
+    return lax.all_to_all(jnp.tile(x, repeats), axis, split_axis=dim, concat_axis=dim, tiled=True)
 
 
 def per_device(train_down, router_weight, router_gain):
@@ -13,7 +19,7 @@
     )
     part_router = (router_weight * router_gain[:, None]).astype(jnp.bfloat16)
     row_router = lax.all_gather(part_router, "shard", axis=0, tiled=True)
-    serve_router = lax.all_gather(row_router, "expert", axis=1, tiled=True)
+    serve_router = tiled_gather(row_router, "expert", 1)
     return (ready_down, scale_down, serve_router)
 
 

time: 508 us -> 487 us (0.959)
  blocking collectives: 329 us -> 18.1 us
  waiting for transfers between devices: 0.01 us -> 283 us
  starting transfers between devices: 8.59 us -> 14.8 us
    all_to_all x1, waiting for transfers between devices: 0.01 us -> 283 us  [per_device(): lax.all_to_all(narrow_down, 'shard', split_axis=1, concat_axis=2, tiled=T...]
    all_gather x1, blocking collectives: 285 us -> 6.25 us  [per_device(): row_router = lax.all_gather(part_router, 'shard', axis=0, tiled=True)]
    all_gather x1 -> x0, blocking collectives: 30.8 us -> none  [per_device(): serve_router = lax.all_gather(row_router, 'expert', axis=1, tiled=True)]
    all_to_all x0 -> x1, starting transfers between devices: none -> 6.22 us  [tiled_gather(): lax.all_to_all(jnp.tile(x, repeats), axis, split_axis=dim, concat_axis=di...]
  transfers between devices with their start and end apart: 1 -> 2, of which waited for: 0 -> 1; matrix products, arithmetic and copies ran while one was open for 0% -> 19% of each run, Pallas kernels for 0% -> 0%
where the time goes in v2:
time: 487 us; the launch traced here: 485 us
  waiting for transfers between devices  283 us (58%)
  local copies, waits for them, and re-layouts  125 us (26%)
  other arithmetic  43.9 us (9%)
  blocking collectives  18.1 us (4%)
  starting transfers between devices  14.8 us (3%)
    all_to_all x1, waiting for transfers between devices, per_device(): lax.all_to_all(narrow_down, 'shard', split_axis=1, concat_axis=2, tiled=T...  283 us
    all_to_all x2, local copies, waits for them, and re-layouts, per_device(): lax.all_to_all(narrow_down, 'shard', split_axis=1, concat_axis=2, tiled=T...  75.8 us
    convert_element_type x1, local copies, waits for them, and re-layouts, per_device(): (train_down / jnp.expand_dims(scale_down, 2)).astype(jnp.bfloat16)  47.3 us
    convert_element_type x1, other arithmetic, per_device(): (train_down / jnp.expand_dims(scale_down, 2)).astype(jnp.bfloat16)  26.1 us
    reduce_max x1, other arithmetic, per_device(): scale_down = lax.pmax(jnp.max(jnp.abs(train_down), axis=2), 'shard')  17 us
    pmax x1, blocking collectives, per_device(): scale_down = lax.pmax(jnp.max(jnp.abs(train_down), axis=2), 'shard')  11.8 us
  transfers between devices with their start and end apart: 2, of which 1 were waited for; matrix products, arithmetic and copies ran while one was open for 19% of the time, Pallas kernels for 0%

profile of v2, /device:TPU:0, one launch (start us, length us, event | category | flops | bytes accessed | tf_op | source)
XLA Modules:
  0.0 485.4 jit_solution(18222184156977529834)
XLA Ops:
  0.6 0.7 multiply_convert_fusion
  1.3 6.3 %all_gather.3 = bf16[4096,2]{0,1:T(2,128)(2,1)S(1)} all-gather(bf16[1024,2]{0,1:T(2,128)(2,1)S(1)} %multiply_convert_fusion), channel_id=1, replica_groups=mesh['expert'=8,'shard'=4] {'shard'}, dimensions={0}, use_global_device_ids=true | all-gather | bytes 20480 | tf_op jit(solution)/shard_map/all_gather | solution.py:21
  7.6 0.7 tile.2
  8.3 6.2 %all-to-all-start.1 = ((bf16[4096,8,2]{0,2,1:T(2,128)(2,1)}), bf16[4096,8,2]{0,2,1:T(2,128)(2,1)S(1)}, u32[]{:S(2)}, u32[]{:S(2)}) async-start(bf16[4096,8,2]{0,2,1:T(2,128)(2,1)} %tile.2), calls=%async_computation.1 | async-start | bytes 262144 | tf_op jit(solution)/shard_map/all_to_all | solution.py:10
  14.5 17.0 %abs_reduce_fusion = f32[2,6400]{1,0:T(2,128)S(1)} fusion(f32[2,6400,1024]{2,1,0:T(8,128)} %param.3), kind=kLoop, calls=%fused_computation.1 | loop fusion | flops 26201600 | bytes 52480000 | tf_op jit(solution)/shard_map/reduce_max | solution.py:14
  31.6 11.8 %pmax.7 = f32[2,6400]{1,0:T(2,128)S(1)} all-reduce(f32[2,6400]{1,0:T(2,128)S(1)} %abs_reduce_fusion), channel_id=1, replica_groups=mesh['expert'=8,'shard'=4] {'shard'}, use_global_device_ids=true, to_apply=%region_1.0 | all-reduce | flops 12800 | bytes 102400 | tf_op jit(solution)/shard_map/pmax | solution.py:14
  43.4 26.1 %divide_convert_fusion = bf16[2,6400,1024]{2,1,0:T(8,128)(2,1)} fusion(f32[2,6400,1024]{2,1,0:T(8,128)} %param.3, f32[2,6400]{1,0:T(2,128)S(1)} %pmax.7), kind=kLoop, calls=%fused_computation | loop fusion | flops 26214400 | bytes 78694400 | tf_op jit(solution)/shard_map/convert_element_type | solution.py:15
  69.5 47.3 %copy.10 = bf16[2,6400,1024]{2,0,1:T(2,128)(2,1)} copy(bf16[2,6400,1024]{2,1,0:T(8,128)(2,1)} %divide_convert_fusion) | data formatting | bytes 52428800 | tf_op jit(solution)/shard_map/convert_element_type | solution.py:15
  116.9 0.0 all-to-all-done.1
  116.9 8.6 %all-to-all-start = ((bf16[2,6400,1024]{2,0,1:T(2,128)(2,1)}), bf16[2,6400,1024]{2,0,1:T(2,128)(2,1)}, u32[]{:S(2)}, u32[]{:S(2)}) async-start(bf16[2,6400,1024]{2,0,1:T(2,128)(2,1)} %copy.10), calls=%async_computation | async-start | bytes 52428800 | tf_op jit(solution)/shard_map/all_to_all | solution.py:16
  125.5 0.7 constant_dynamic-slice_fusion
  126.2 0.7 all_to_all.24
  126.9 282.7 %all-to-all-done = bf16[2,6400,1024]{2,0,1:T(2,128)(2,1)} async-done(((bf16[2,6400,1024]{2,0,1:T(2,128)(2,1)}), bf16[2,6400,1024]{2,0,1:T(2,128)(2,1)}, u32[]{:S(2)}, u32[]{:S(2)}) %all-to-all-start) | async-done | bytes 26214432 | tf_op jit(solution)/shard_map/all_to_all | solution.py:16
  409.6 33.3 %copy.11 = bf16[2,1600,4,1024]{3,2,1,0:T(4,128)(2,1)} copy(bf16[2,1600,4,1024]{3,0,1,2:T(2,128)(2,1)} %bitcast.1) | data formatting | bytes 52428800 | tf_op jit(solution)/shard_map/all_to_all | solution.py:16
  443.0 42.5 %all_to_all.22 = bf16[2,1600,4096]{2,1,0:T(8,128)(2,1)} reshape(bf16[2,1600,4,1024]{3,2,1,0:T(4,128)(2,1)} %copy.11) | data formatting | bytes 52428800 | tf_op jit(solution)/shard_map/all_to_all | solution.py:16
Async XLA Ops:
  8.3 108.5 %all-to-all-start.1 = ((bf16[4096,8,2]{0,2,1:T(2,128)(2,1)}), bf16[4096,8,2]{0,2,1:T(2,128)(2,1)S(1)}, u32[]{:S(2)}, u32[]{:S(2)}) async-start(bf16[4096,8,2]{0,2,1:T(2,128)(2,1)} %tile.2), calls=%async_computation.1 | async-start | bytes 262144 | tf_op jit(solution)/shard_map/all_to_all | solution.py:10
  116.9 292.8 %all-to-all-start = ((bf16[2,6400,1024]{2,0,1:T(2,128)(2,1)}), bf16[2,6400,1024]{2,0,1:T(2,128)(2,1)}, u32[]{:S(2)}, u32[]{:S(2)}) async-start(bf16[2,6400,1024]{2,0,1:T(2,128)(2,1)} %copy.10), calls=%async_computation | async-start | bytes 52428800 | tf_op jit(solution)/shard_map/all_to_all | solution.py:16
